TPU v7x, 16 devices: a 4x2x1 block of a 4x4x8 slice. The times are simulated.
16 devices in a mesh: dp: 2 (over y, z), sp: 8 (over x, core).
Axes of the slice: x: 4, y: 2, z: 1, core: 2. Of those that a mesh axis runs over, the one named last changes fastest.
The devices are a block of a 4x4x8 slice.
Arguments:
- q: bfloat16 [64, 16, 64], P('dp'), parts along dimension 0
- k: bfloat16 [64, 8192, 16, 64], P('dp', 'sp'), parts along dimension 0
- v: bfloat16 [64, 8192, 16, 64], P('dp', 'sp'), parts along dimension 0
Outputs:
- q: bfloat16 [64, 16, 64], P('dp'), parts along dimension 0
There are 2 independent parts. A program takes and returns all parts, laid end to end along the dimension named above; each array names one.
All inputs are finite; a program needn't handle non-finite values.
Results may differ from a plain program's by a relative error of at most 0.012.
Values are sent between devices in bfloat16 or wider.
A program may use at most 768 MiB of HBM per device.

v0:
```python
import jax
import jax.numpy as jnp
from jax import lax
from jax.sharding import PartitionSpec as P


def einsum(form, a, b):
    return jnp.einsum(form, a.astype(jnp.float32), b.astype(jnp.float32))


def part_of(q, k, v):
    grouped = q.reshape(q.shape[0], k.shape[2], -1, q.shape[2])
    scores = einsum("bgsd,bugd->bgsu", grouped, k) * q.shape[2] ** -0.5
    high = jnp.max(scores, -1, keepdims=True)
    weights = jnp.exp(scores - high)
    seen = einsum("bgsu,bugd->bgsd", weights.astype(jnp.bfloat16), v)
    return jnp.concatenate([seen, jnp.sum(weights, -1, keepdims=True), high], -1)


def together(parts):
    seen, total, high = parts[..., :-2], parts[..., -2:-1], parts[..., -1:]
    scale = jnp.exp(high - jnp.max(high, 0))
    return (jnp.sum(seen * scale, 0) / jnp.sum(total * scale, 0)).astype(jnp.bfloat16)


def solution(mesh):
    def step(q, k, v):
        return together(lax.all_gather(part_of(q, k, v), "sp")).reshape(q.shape)

    return jax.shard_map(
        step,
        mesh=mesh,
        in_specs=(P("dp", None, None), P("dp", "sp", None, None), P("dp", "sp", None, None)),
        out_specs=P("dp", None, None),
        check_vma=False,
    )
```

profile of v0, /device:TPU:113, one launch (start us, length us, event | category | flops | bytes accessed | tf_op | source)
XLA Modules:
  0.0 98.7 jit_solution(4038899605279839550)
XLA Ops:
  6.5 0.0 all-gather.3.cloned.1.call-start
  6.6 22.7 %fusion.8 = f32[32,16,1,1024]{3,2,1,0:T(1,128)S(1)} fusion(bf16[32,1024,16,64]{1,3,2,0:T(8,128)(2,1)} %param.4, bf16[32,16,64,1]{2,1,0,3:T(8,128)(2,1)} %bitcast.26), kind=kOutput, calls=%fused_computation.15 | convolution fusion | flops 67108864 | bytes 69271552 | tf_op jit(solution)/shard_map/bgsd,bugd->bgsu/dot_general | solution.py:8
  29.3 0.5 fusion.6
  29.7 0.7 fusion.7
  30.4 0.3 copy.23
  30.7 0.3 copy.22
  30.9 25.7 %fusion.2 = f32[32,16,1,64]{3,2,1,0:T(1,128)S(1)} fusion(bf16[32,1024,16,64]{1,3,2,0:T(8,128)(2,1)} %param.5, bf16[32,16,1024,1]{2,1,0,3:T(8,128)(2,1)S(1)} %get-tuple-element.7), kind=kOutput, calls=%fused_computation.5 | convolution fusion | flops 67108864 | bytes 68288512 | tf_op jit(solution)/shard_map/bgsu,bugd->bgsd/dot_general | solution.py:8
  56.7 0.9 pad_maximum_fusion
  57.6 0.1 all-gather.3.cloned.1.call-update
  57.6 24.4 %all-gather.3.cloned.1.call-done = f32[256,16,1,66]{3,1,2,0:T(8,128)} async-done(((f32[32,16,1,66]{3,1,2,0:T(8,128)}), f32[256,16,1,66]{3,1,2,0:T(8,128)}) %all-gather.3.cloned.1.call-update) | async-done | bytes 1081360 | tf_op jit(solution)/shard_map/all_gather | solution.py:28
  82.1 0.0 copy-start
  82.1 2.4 %slice_reduce_fusion = f32[32,16]{1,0:T(8,128)S(1)} fusion(f32[8,32,16,1,66]{4,2,1,0,3:T(8,128)} %bitcast.23), kind=kLoop, calls=%fused_computation.9 | loop fusion | flops 3584 | bytes 18432 | tf_op jit(solution)/shard_map/reduce_max | solution.py:22
  84.5 0.0 copy-done
  84.5 2.6 %fusion = (f32[32,16]{1,0:T(8,128)S(1)}, f32[8,32,16,1,1]{4,2,1,0,3:T(8,128)}) fusion(f32[8,32,16,1,66]{4,2,1,0,3:T(8,128)S(1)} %bitcast.24, f32[32,16]{1,0:T(8,128)S(1)} %slice_reduce_fusion), kind=kLoop, calls=%fused_computation.1 | loop fusion | flops 11776 | bytes 53248 | tf_op jit(solution)/shard_map/reduce_sum | solution.py:23
  87.1 3.1 %copy.34 = f32[8,32,16,1,1]{2,1,0,3,4:T(8,128)S(1)} copy(f32[8,32,16,1,1]{4,2,1,0,3:T(8,128)} %get-tuple-element.6) | data formatting | bytes 32768 | tf_op jit(solution)/shard_map/mul | solution.py:23
  90.2 0.8 fusion.1
  91.0 0.8 divide_convert_fusion
Async XLA Ops:
  6.5 75.5 %all-gather.3.cloned.1.call-start = ((), (), s32[]{:S(2)}) async-start(), calls=%async_computation | async-start | bytes 2359296 | tf_op jit(solution)/shard_map/all_gather | solution.py:28
  82.1 2.4 %copy-start = (f32[256,16,1,66]{3,1,2,0:T(8,128)S(1)}, f32[256,16,1,66]{3,1,2,0:T(8,128)}, u32[]{:S(2)}) copy-start(f32[256,16,1,66]{3,1,2,0:T(8,128)} %all-gather.3.cloned.1.call-done) | copy-start | bytes 3244036
Sparse Core Ops, SparseCore 0:
  57.8 24.2 all-gather.2
where the time goes:
time: 98.9 us; the launch traced here: 98.7 us
  matrix products  48.4 us (49%)
  waiting for transfers between devices  24.5 us (25%)
  between operations  13.5 us (14%)
  other arithmetic  8.63 us (9%)
  local copies, waits for them, and re-layouts  3.66 us (4%)
    dot_general x2, matrix products, einsum(): return jnp.einsum(form, a.astype(jnp.float32), b.astype(jnp.float32))  48.4 us
    all_gather x1, waiting for transfers between devices, step(): return together(lax.all_gather(part_of(q, k, v), 'sp')).reshape(q.shape)  24.4 us
    mul x1, local copies, waits for them, and re-layouts, together(): seen * scale  3.13 us
    reduce_sum x1, other arithmetic, together(): jnp.sum(total * scale, 0)  2.58 us
    reduce_max x1, other arithmetic, together(): scale = jnp.exp(high - jnp.max(high, 0))  2.44 us
  transfers between devices with their start and end apart: 1, of which 1 were waited for; matrix products, arithmetic and copies ran while one was open for 0% of the time, Pallas kernels for 0%

commit v1 on v0

v1 whole, which is shorter than its diff:
```python
import functools

import jax
import jax.numpy as jnp
from jax import lax
from jax.experimental import pallas as pl
from jax.experimental.pallas import tpu as pltpu
from jax.sharding import PartitionSpec as P

SLOTS = 5
LAG = 4


def kernel(n, scale, q_ref, k_hbm, v_hbm, out_ref, k_buf, v_buf, parts, k_sem, v_sem, send_sem, recv_sem):
    me = lax.axis_index("sp")
    seqs, heads, head = q_ref.shape
    width = heads * head

    def fetch_k(s, slot):
        return pltpu.make_async_copy(k_hbm.at[s], k_buf.at[slot], k_sem.at[slot])

    def fetch_v(s, slot):
        return pltpu.make_async_copy(v_hbm.at[s], v_buf.at[slot], v_sem.at[slot])

    for s in range(SLOTS):
        fetch_k(s, s).start()
        fetch_v(s, s).start()

    barrier = pltpu.get_barrier_semaphore()
    for d in range(1, n):
        pl.semaphore_signal(barrier, inc=1, device_id={"sp": lax.rem(me + d, n)})

    def weights_of(s, slot):
        q = q_ref[s]
        row = lax.broadcasted_iota(jnp.int32, (heads, width), 0)
        owner = lax.broadcasted_iota(jnp.int32, (heads, width), 1) // head
        diagonal = jnp.where(owner == row, jnp.concatenate([q] * heads, axis=1), jnp.zeros((), q.dtype))
        scores = jnp.dot(diagonal, k_buf[slot], preferred_element_type=jnp.float32) * scale
        high = jnp.max(scores, -1, keepdims=True)
        weights = jnp.exp(scores - high)
        return weights.astype(v_buf.dtype), jnp.sum(weights, -1, keepdims=True), high

    lane = lax.broadcasted_iota(jnp.int32, (heads, 128), 1)
    row = lax.broadcasted_iota(jnp.int32, (heads, 128), 0)

    def part_of(slot, weights, total, high):
        every = lax.dot_general(weights, v_buf[slot], (((1,), (1,)), ((), ())), preferred_element_type=jnp.float32)
        seen = jnp.zeros((heads, 128), jnp.float32)
        per = 128 // head
        for j in range(width // 128):
            seen = jnp.where(lane // head + per * j == row, every[:, 128 * j : 128 * j + 128], seen)
        seen = jnp.where(lane // head == lax.rem(row, per), seen, 0.0)
        seen = seen + pltpu.roll(seen, head, 1)
        return jnp.where(lane < head, seen, jnp.where(lane < head + head // 2, total, high))

    def send(s):
        for d in range(1, n):
            pltpu.make_async_remote_copy(
                src_ref=parts.at[me, s],
                dst_ref=parts.at[me, s],
                send_sem=send_sem,
                recv_sem=recv_sem.at[s],
                device_id={"sp": lax.rem(me + d, n)},
            ).start()

    def combine(s):
        pltpu.make_async_copy(parts.at[pl.ds(0, n - 1), s], parts.at[pl.ds(0, n - 1), s], recv_sem.at[s]).wait()
        tiles = [parts[p, s] for p in range(n)]
        highs = [jnp.broadcast_to(t[:, 127:128], t.shape) for t in tiles]
        top = functools.reduce(jnp.maximum, highs)
        both = functools.reduce(jnp.add, [t * jnp.exp(h - top) for t, h in zip(tiles, highs)])
        out_ref[s] = (both / jnp.broadcast_to(both[:, head : head + 1], both.shape))[:, :head].astype(out_ref.dtype)

    fetch_k(0, 0).wait()
    state = weights_of(0, 0)
    pl.semaphore_wait(barrier, n - 1)

    def step(s, state):
        slot, before = lax.rem(s, SLOTS), lax.rem(s - 1, SLOTS)
        fetch_k(s, slot).wait()
        fetch_v(s - 1, before).wait()
        parts[me, s - 1] = part_of(before, *state)
        state = weights_of(s, slot)

        @pl.when(s - 1 + SLOTS < seqs)
        def _():
            fetch_v(s - 1 + SLOTS, before).start()

        @pl.when(s + SLOTS < seqs)
        def _():
            fetch_k(s + SLOTS, slot).start()

        send(s - 1)

        @pl.when(s > LAG)
        def _():
            combine(s - 1 - LAG)

        return state

    fetch_k(SLOTS, 0).start()
    state = lax.fori_loop(1, seqs, step, state)

    last = seqs - 1
    fetch_v(last, last % SLOTS).wait()
    parts[me, last] = part_of(last % SLOTS, *state)
    send(last)
    for s in range(seqs - 1 - LAG, seqs):
        combine(s)
    pltpu.make_async_copy(parts.at[pl.ds(0, n - 1)], parts.at[pl.ds(0, n - 1)], send_sem).wait()


def solution(mesh):
    n = mesh.shape["sp"]

    def step(q, k, v):
        seqs, tokens, heads, head = k.shape
        k = jnp.transpose(k, (0, 2, 3, 1)).reshape(seqs, heads * head, tokens)
        v = jnp.transpose(v, (0, 2, 3, 1)).reshape(seqs, heads * head, tokens)
        return pl.pallas_call(
            functools.partial(kernel, n, head**-0.5),
            out_shape=jax.ShapeDtypeStruct(q.shape, q.dtype),
            in_specs=[
                pl.BlockSpec(memory_space=pltpu.VMEM),
                pl.BlockSpec(memory_space=pl.ANY),
                pl.BlockSpec(memory_space=pl.ANY),
            ],
            out_specs=pl.BlockSpec(memory_space=pltpu.VMEM),
            scratch_shapes=[
                pltpu.VMEM((SLOTS, heads * head, tokens), k.dtype),
                pltpu.VMEM((SLOTS, heads * head, tokens), v.dtype),
                pltpu.VMEM((n, seqs, heads, 128), jnp.float32),
                pltpu.SemaphoreType.DMA((SLOTS,)),
                pltpu.SemaphoreType.DMA((SLOTS,)),
                pltpu.SemaphoreType.DMA,
                pltpu.SemaphoreType.DMA((seqs,)),
            ],
            compiler_params=pltpu.CompilerParams(collective_id=0, has_side_effects=True, vmem_limit_bytes=60 * 1024 * 1024),
            cost_estimate=pl.CostEstimate(
                flops=4 * seqs * tokens * heads * head,
                bytes_accessed=2 * k.size * k.dtype.itemsize,
                transcendentals=seqs * heads * tokens,
            ),
        )(q, k, v)

    return jax.shard_map(
        step,
        mesh=mesh,
        in_specs=(P("dp", None, None), P("dp", "sp", None, None), P("dp", "sp", None, None)),
        out_specs=P("dp", None, None),
        check_vma=False,
    )
```

time: 98.9 us -> 54.8 us (0.55)
  Pallas kernels: 0 us -> 53.1 us
  matrix products: 48.4 us -> 0 us
  waiting for transfers between devices: 24.5 us -> 0 us
  between operations: 13.5 us -> 0.01 us
  other arithmetic: 8.63 us -> 0 us
  local copies, waits for them, and re-layouts: 3.66 us -> 1.57 us
    pallas_call x0 -> x1, Pallas kernels: none -> 53.1 us  [step(): pl.pallas_call(functools.partial(kernel, n, head ** (-0.5)), out_shape=ja...]
    dot_general x2 -> x0, matrix products: 48.4 us -> none  [einsum(): return jnp.einsum(form, a.astype(jnp.float32), b.astype(jnp.float32))]
    all_gather x1 -> x0, waiting for transfers between devices: 24.4 us -> none  [step(): return together(lax.all_gather(part_of(q, k, v), 'sp')).reshape(q.shape)]
    reduce_sum x2 -> x0, other arithmetic: 3.33 us -> none  [the longest x1 2.58 us: together(): jnp.sum(total * scale, 0)]
    mul x1 -> x0, local copies, waits for them, and re-layouts: 3.13 us -> none  [together(): seen * scale]
    reduce_max x2 -> x0, other arithmetic: 2.9 us -> none  [the longest x1 2.44 us: together(): scale = jnp.exp(high - jnp.max(high, 0))]
    unnamed x2 -> x1, local copies, waits for them, and re-layouts: 0.01 us -> 1.57 us
    convert_element_type x2 -> x0, other arithmetic: 1.47 us -> none  [the longest x1 0.8 us: together(): (jnp.sum(seen * scale, 0) / jnp.sum(total * scale, 0)).astype(jnp.bfloat16)]
  transfers between devices with their start and end apart: 1 -> 0, of which waited for: 1 -> 0; matrix products, arithmetic and copies ran while one was open for 0% -> 0% of each run, Pallas kernels for 0% -> 0%
where the time goes in v1:
time: 54.8 us; the launch traced here: 54.7 us
  Pallas kernels  53.1 us (97%)
  local copies, waits for them, and re-layouts  1.57 us (3%)
    pallas_call x1, Pallas kernels, step(): pl.pallas_call(functools.partial(kernel, n, head ** (-0.5)), out_shape=ja...  53.1 us
    unnamed x1, local copies, waits for them, and re-layouts  1.57 us

profile of v1, /device:TPU:113, one launch (start us, length us, event | category | flops | bytes accessed | tf_op | source)
XLA Modules:
  0.0 54.7 jit_solution(2547515935725281531)
XLA Ops:
  0.0 53.1 %shard_map.37 = bf16[32,16,64]{2,1,0:T(8,128)(2,1)} custom-call(bf16[32,16,64]{2,1,0:T(8,128)(2,1)} %q_ref.1, bf16[32,1024,1024]{2,1,0:T(8,128)(2,1)} %bitcast.1.k_hbm, bf16[32,1024,1024]{2,1,0:T(8,128)(2,1)} %bitcast.3.v_hbm), custom_call_target="tpu_custom_call" | custom-call | flops 134217728 | bytes 134217728 | tf_op jit(solution)/shard_map/pallas_call | solution.py:120
  53.1 1.6 %copy.5 = bf16[32,16,64]{2,1,0:T(8,128)(2,1)} copy(bf16[32,16,64]{2,1,0:T(8,128)(2,1)} %shard_map.37) | data formatting | bytes 131072

commit v2 on v1

v2 whole, which is shorter than its diff:
```python
import functools

import jax
import jax.numpy as jnp
from jax import lax
from jax.experimental import pallas as pl
from jax.experimental.pallas import tpu as pltpu
from jax.sharding import PartitionSpec as P

SLOTS = 4
LAG = 4


def kernel(n, scale, q_hbm, k_hbm, v_hbm, out_ref, q_ref, k_buf, v_buf, parts, q_sem, k_sem, v_sem, send_sem, recv_sem):
    me = lax.axis_index("sp")
    seqs, heads, head = q_ref.shape
    width = heads * head

    def fetch_k(s, slot):
        return pltpu.make_async_copy(k_hbm.at[s], k_buf.at[slot], k_sem.at[slot])

    def fetch_v(s, slot):
        return pltpu.make_async_copy(v_hbm.at[s], v_buf.at[slot], v_sem.at[slot])

    fetch_q = pltpu.make_async_copy(q_hbm, q_ref, q_sem)
    fetch_q.start()
    for s in range(SLOTS):
        fetch_k(s, s).start(priority=1)
        fetch_v(s, s).start(priority=1)

    barrier = pltpu.get_barrier_semaphore()
    for d in range(1, n):
        pl.semaphore_signal(barrier, inc=1, device_id={"sp": lax.rem(me + d, n)})

    def weights_of(s, slot):
        q = q_ref[s]
        row = lax.broadcasted_iota(jnp.int32, (heads, width), 0)
        owner = lax.broadcasted_iota(jnp.int32, (heads, width), 1) // head
        diagonal = jnp.where(owner == row, jnp.concatenate([q] * heads, axis=1), jnp.zeros((), q.dtype))
        scores = jnp.dot(diagonal, k_buf[slot], preferred_element_type=jnp.float32) * scale
        high = jnp.max(scores, -1, keepdims=True)
        weights = jnp.exp(scores - high)
        return weights.astype(v_buf.dtype), jnp.sum(weights, -1, keepdims=True), high

    lane = lax.broadcasted_iota(jnp.int32, (heads, 128), 1)
    row = lax.broadcasted_iota(jnp.int32, (heads, 128), 0)
    per = 128 // head

    def part_of(slot, weights, total, high):
        every = lax.dot_general(weights, v_buf[slot], (((1,), (1,)), ((), ())), preferred_element_type=jnp.float32)
        seen = jnp.zeros((heads, 128), jnp.float32)
        for j in range(width // 128):
            seen = jnp.where(lane // head + per * j == row, every[:, 128 * j : 128 * j + 128], seen)
        seen = seen + pltpu.roll(seen, head, 1)
        return jnp.where(lane < head, seen, jnp.where(lane < head + head // 2, total, high))

    def send(s):
        place = parts.at[me, s]
        for d in sorted(range(1, n), key=lambda d: -min(d, n - d)):
            pltpu.make_async_remote_copy(
                src_ref=place,
                dst_ref=place,
                send_sem=send_sem,
                recv_sem=recv_sem.at[s],
                device_id={"sp": lax.rem(me + d, n)},
            ).start()

    def wait_parts(s):
        place = parts.at[pl.ds(0, n - 1), s]
        pltpu.make_async_copy(place, place, recv_sem.at[s]).wait()

    def combine(s):
        tiles = [parts[p, s] for p in range(n)]
        highs = [jnp.broadcast_to(t[:, 127:128], t.shape) for t in tiles]
        top = functools.reduce(jnp.maximum, highs)
        both = functools.reduce(jnp.add, [t * jnp.exp(h - top) for t, h in zip(tiles, highs)])
        result = both / jnp.broadcast_to(both[:, head : head + 1], both.shape)
        out_ref[s] = result[:, :head].astype(out_ref.dtype)

    def block(s, state):
        slot, after = lax.rem(s, SLOTS), lax.rem(s + 1, SLOTS)
        coming = weights_of(s + 1, after)
        parts[me, s] = part_of(slot, *state)

        @pl.when(s + SLOTS < seqs)
        def _():
            fetch_v(s + SLOTS, slot).start(priority=1)

        @pl.when(s + 1 + SLOTS < seqs)
        def _():
            fetch_k(s + 1 + SLOTS, after).start(priority=1)

        return coming

    def need(s):
        fetch_k(s + 1, lax.rem(s + 1, SLOTS)).wait()
        fetch_v(s, lax.rem(s, SLOTS)).wait()

    fetch_q.wait()
    fetch_k(0, 0).wait()
    state = weights_of(0, 0)
    fetch_k(SLOTS, 0).start(priority=1)
    pl.semaphore_wait(barrier, n - 1)
    need(0)
    state = block(0, state)

    def early(s, state):
        need(s)
        send(s - 1)
        return block(s, state)

    def later(s, state):
        wait_parts(s - 1 - LAG)
        need(s)
        send(s - 1)
        combine(s - 1 - LAG)
        return block(s, state)

    last = seqs - 1
    state = lax.fori_loop(1, 1 + LAG, early, state)
    state = lax.fori_loop(1 + LAG, last - 1, later, state)

    send(last - 2)
    fetch_v(last - 1, (last - 1) % SLOTS).wait()
    parts[me, last - 1] = part_of((last - 1) % SLOTS, *state)
    fetch_k(last, last % SLOTS).wait()
    state = weights_of(last, last % SLOTS)
    send(last - 1)
    fetch_v(last, last % SLOTS).wait()
    parts[me, last] = part_of(last % SLOTS, *state)
    send(last)
    for s in range(last - 2 - LAG, seqs):
        wait_parts(s)
        combine(s)
    pltpu.make_async_copy(parts.at[pl.ds(0, n - 1)], parts.at[pl.ds(0, n - 1)], send_sem).wait()


def solution(mesh):
    n = mesh.shape["sp"]

    def step(q, k, v):
        seqs, tokens, heads, head = k.shape
        k = jnp.transpose(k, (0, 2, 3, 1)).reshape(seqs, heads * head, tokens)
        v = jnp.transpose(v, (0, 2, 3, 1)).reshape(seqs, heads * head, tokens)
        return pl.pallas_call(
            functools.partial(kernel, n, head**-0.5),
            out_shape=jax.ShapeDtypeStruct(q.shape, q.dtype),
            in_specs=[pl.BlockSpec(memory_space=pl.ANY)] * 3,
            out_specs=pl.BlockSpec(memory_space=pltpu.VMEM),
            scratch_shapes=[
                pltpu.VMEM(q.shape, q.dtype),
                pltpu.VMEM((SLOTS, heads * head, tokens), k.dtype),
                pltpu.VMEM((SLOTS, heads * head, tokens), v.dtype),
                pltpu.VMEM((n, seqs, heads, 128), jnp.float32),
                pltpu.SemaphoreType.DMA,
                pltpu.SemaphoreType.DMA((SLOTS,)),
                pltpu.SemaphoreType.DMA((SLOTS,)),
                pltpu.SemaphoreType.DMA,
                pltpu.SemaphoreType.DMA((seqs,)),
            ],
            compiler_params=pltpu.CompilerParams(
                collective_id=0, has_side_effects=True, vmem_limit_bytes=30 * 1024 * 1024
            ),
            cost_estimate=pl.CostEstimate(
                flops=4 * seqs * tokens * heads * head,
                bytes_accessed=2 * k.size * k.dtype.itemsize,
                transcendentals=seqs * heads * tokens,
            ),
        )(pltpu.with_memory_space_constraint(q, pltpu.HBM), k, v)

    return jax.shard_map(
        step,
        mesh=mesh,
        in_specs=(P("dp", None, None), P("dp", "sp", None, None), P("dp", "sp", None, None)),
        out_specs=P("dp", None, None),
        check_vma=False,
    )
```

time: 54.8 us -> 48.4 us (0.88)
  Pallas kernels: 53.1 us -> 47.7 us
  local copies, waits for them, and re-layouts: 1.57 us -> 0.66 us
    pallas_call x1, Pallas kernels: 53.1 us -> 47.7 us  [step(): pl.pallas_call(functools.partial(kernel, n, head ** (-0.5)), out_shape=ja...]
    unnamed x1, local copies, waits for them, and re-layouts: 1.57 us -> 0.66 us
where the time goes in v2:
time: 48.4 us; the launch traced here: 48.3 us
  Pallas kernels  47.7 us (99%)
  local copies, waits for them, and re-layouts  0.66 us (1%)
    pallas_call x1, Pallas kernels, step(): pl.pallas_call(functools.partial(kernel, n, head ** (-0.5)), out_shape=ja...  47.7 us

profile of v2, /device:TPU:113, one launch (start us, length us, event | category | flops | bytes accessed | tf_op | source)
XLA Modules:
  0.0 48.3 jit_solution(5301384662111013847)
XLA Ops:
  0.0 47.7 %shard_map.37 = bf16[32,16,64]{2,1,0:T(8,128)(2,1)S(1)} custom-call(bf16[32,16,64]{2,1,0:T(8,128)(2,1)} %q_hbm.1, bf16[32,1024,1024]{2,1,0:T(8,128)(2,1)} %bitcast.1.k_hbm, bf16[32,1024,1024]{2,1,0:T(8,128)(2,1)} %bitcast.3.v_hbm), custom_call_target="tpu_custom_call" | custom-call | flops 134217728 | bytes 134217728 | tf_op jit(solution)/shard_map/pallas_call | solution.py:145
  47.7 0.7 %copy.5 = bf16[32,16,64]{2,1,0:T(8,128)(2,1)} copy(bf16[32,16,64]{2,1,0:T(8,128)(2,1)S(1)} %shard_map.37) | data formatting | bytes 131072

commit v3 on v2

--- a/solution.py
+++ b/solution.py
@@ -8,6 +8,7 @@
 from jax.sharding import PartitionSpec as P
 
 SLOTS = 4
+ASIDE = 8
 LAG = 4
 
 
@@ -24,9 +25,10 @@
 
     fetch_q = pltpu.make_async_copy(q_hbm, q_ref, q_sem)
     fetch_q.start()
-    for s in range(SLOTS):
+    fetch_k(0, 0).start(priority=1)
+    for s in range(1, SLOTS):
         fetch_k(s, s).start(priority=1)
-        fetch_v(s, s).start(priority=1)
+        fetch_v(s - 1, s - 1).start(priority=1)
 
     barrier = pltpu.get_barrier_semaphore()
     for d in range(1, n):
@@ -47,11 +49,23 @@
     per = 128 // head
 
     def part_of(slot, weights, total, high):
-        every = lax.dot_general(weights, v_buf[slot], (((1,), (1,)), ((), ())), preferred_element_type=jnp.float32)
+        cut = (heads - ASIDE) * head
+        every = lax.dot_general(weights, v_buf[slot, :cut], (((1,), (1,)), ((), ())), preferred_element_type=jnp.float32)
         seen = jnp.zeros((heads, 128), jnp.float32)
-        for j in range(width // 128):
+        for j in range(cut // 128):
             seen = jnp.where(lane // head + per * j == row, every[:, 128 * j : 128 * j + 128], seen)
         seen = seen + pltpu.roll(seen, head, 1)
+        wide = weights.astype(jnp.float32)
+        column = lax.broadcasted_iota(jnp.int32, (head, 128), 1)
+        turned = jnp.zeros((head, 128), jnp.float32)
+        for h in range(heads - ASIDE, heads):
+            terms = [
+                v_buf[slot, h * head : (h + 1) * head, t : t + 128].astype(jnp.float32) * wide[h : h + 1, t : t + 128]
+                for t in range(0, wide.shape[1], 128)
+            ]
+            turned = jnp.where(column == h, jnp.sum(functools.reduce(jnp.add, terms), 1, keepdims=True), turned)
+        turned = turned.T[:heads]
+        seen = seen + jnp.concatenate([turned, turned], 1)
         return jnp.where(lane < head, seen, jnp.where(lane < head + head // 2, total, high))
 
     def send(s):
@@ -82,13 +96,13 @@
         coming = weights_of(s + 1, after)
         parts[me, s] = part_of(slot, *state)
 
+        @pl.when(s + 1 + SLOTS < seqs)
+        def _():
+            fetch_k(s + 1 + SLOTS, after).start(priority=1)
+
         @pl.when(s + SLOTS < seqs)
         def _():
             fetch_v(s + SLOTS, slot).start(priority=1)
-
-        @pl.when(s + 1 + SLOTS < seqs)
-        def _():
-            fetch_k(s + 1 + SLOTS, after).start(priority=1)
 
         return coming
 
@@ -100,6 +114,7 @@
     fetch_k(0, 0).wait()
     state = weights_of(0, 0)
     fetch_k(SLOTS, 0).start(priority=1)
+    fetch_v(SLOTS - 1, SLOTS - 1).start(priority=1)
     pl.semaphore_wait(barrier, n - 1)
     need(0)
     state = block(0, state)
@@ -121,10 +136,11 @@
     state = lax.fori_loop(1 + LAG, last - 1, later, state)
 
     send(last - 2)
+    fetch_k(last, last % SLOTS).wait()
+    coming = weights_of(last, last % SLOTS)
     fetch_v(last - 1, (last - 1) % SLOTS).wait()
     parts[me, last - 1] = part_of((last - 1) % SLOTS, *state)
-    fetch_k(last, last % SLOTS).wait()
-    state = weights_of(last, last % SLOTS)
+    state = coming
     send(last - 1)
     fetch_v(last, last % SLOTS).wait()
     parts[me, last] = part_of(last % SLOTS, *state)

time: 48.4 us -> 47.9 us (0.990)
  Pallas kernels: 47.7 us -> 47.2 us
where the time goes in v3:
time: 47.9 us
  Pallas kernels  47.2 us (99%)
  local copies, waits for them, and re-layouts  0.66 us (1%)
    pallas_call x1, Pallas kernels, step(): pl.pallas_call(functools.partial(kernel, n, head ** (-0.5)), out_shape=ja...  47.2 us

profile of v3, /device:TPU:113, one launch (start us, length us, event | category | flops | bytes accessed | tf_op | source)
XLA Modules:
  0.0 47.9 jit_solution(6189450128536135260)
XLA Ops:
  0.0 47.2 %shard_map.37 = bf16[32,16,64]{2,1,0:T(8,128)(2,1)S(1)} custom-call(bf16[32,16,64]{2,1,0:T(8,128)(2,1)} %q_hbm.1, bf16[32,1024,1024]{2,1,0:T(8,128)(2,1)} %bitcast.1.k_hbm, bf16[32,1024,1024]{2,1,0:T(8,128)(2,1)} %bitcast.3.v_hbm), custom_call_target="tpu_custom_call" | custom-call | flops 134217728 | bytes 134217728 | tf_op jit(solution)/shard_map/pallas_call | solution.py:161
  47.2 0.7 %copy.5 = bf16[32,16,64]{2,1,0:T(8,128)(2,1)} copy(bf16[32,16,64]{2,1,0:T(8,128)(2,1)S(1)} %shard_map.37) | data formatting | bytes 131072

commit v4 on v3

v4 whole, which is shorter than its diff:
```python
import functools

import jax
import jax.numpy as jnp
from jax import lax
from jax.experimental import pallas as pl
from jax.experimental.pallas import tpu as pltpu
from jax.sharding import PartitionSpec as P

SLOTS = 3
ASIDE = 8
LAG = 7
BATCH = 4


def kernel(n, scale, q_hbm, k_hbm, v_hbm, out_ref, q_ref, k_buf, v_buf, parts, q_sem, k_sem, v_sem, send_sem, recv_sem):
    me = lax.axis_index("sp")
    seqs, heads, head = q_ref.shape
    width = heads * head
    last = seqs - 1

    def fetch_k(s):
        slot = lax.rem(s, SLOTS)
        return pltpu.make_async_copy(k_hbm.at[s], k_buf.at[slot], k_sem.at[slot])

    def fetch_v(s):
        slot = lax.rem(s, SLOTS)
        return pltpu.make_async_copy(v_hbm.at[s], v_buf.at[slot], v_sem.at[slot])

    for copy in fetch_k(0), fetch_k(1), fetch_v(0), fetch_k(2), fetch_v(1):
        copy.start(priority=1)
    fetch_q = pltpu.make_async_copy(q_hbm, q_ref, q_sem)
    fetch_q.start()

    barrier = pltpu.get_barrier_semaphore()
    for d in range(1, n):
        pl.semaphore_signal(barrier, inc=1, device_id={"sp": lax.rem(me + d, n)})

    def need(s):
        fetch_k(s + 1).wait()

        @pl.when(s + 3 < seqs)
        def _():
            fetch_k(s + 3).start(priority=1)

        fetch_v(s).wait()

        @pl.when(s + 2 < seqs)
        def _():
            fetch_v(s + 2).start(priority=1)

    def weights_of(s):
        q = q_ref[s]
        row = lax.broadcasted_iota(jnp.int32, (heads, width), 0)
        owner = lax.broadcasted_iota(jnp.int32, (heads, width), 1) // head
        diagonal = jnp.where(owner == row, jnp.concatenate([q] * heads, axis=1), jnp.zeros((), q.dtype))
        scores = jnp.dot(diagonal, k_buf[lax.rem(s, SLOTS)], preferred_element_type=jnp.float32) * scale
        high = jnp.max(scores, -1, keepdims=True)
        weights = jnp.exp(scores - high)
        return weights.astype(v_buf.dtype), jnp.sum(weights, -1, keepdims=True), high

    lane = lax.broadcasted_iota(jnp.int32, (heads, 128), 1)
    row = lax.broadcasted_iota(jnp.int32, (heads, 128), 0)
    per = 128 // head

    def seen_of(s, weights):
        slot, cut = lax.rem(s, SLOTS), (heads - ASIDE) * head
        every = lax.dot_general(
            weights, v_buf[slot, :cut], (((1,), (1,)), ((), ())), preferred_element_type=jnp.float32
        )
        seen = jnp.zeros((heads, 128), jnp.float32)
        for j in range(cut // 128):
            seen = jnp.where(lane // head + per * j == row, every[:, 128 * j : 128 * j + 128], seen)
        seen = seen + pltpu.roll(seen, head, 1)
        wide = weights.astype(jnp.float32)
        column = lax.broadcasted_iota(jnp.int32, (head, 128), 1)
        turned = jnp.zeros((head, 128), jnp.float32)
        for h in range(heads - ASIDE, heads):
            terms = [
                v_buf[slot, h * head : (h + 1) * head, t : t + 128].astype(jnp.float32) * wide[h : h + 1, t : t + 128]
                for t in range(0, wide.shape[1], 128)
            ]
            turned = jnp.where(column == h, jnp.sum(functools.reduce(jnp.add, terms), 1, keepdims=True), turned)
        turned = turned.T[:heads]
        return seen + jnp.concatenate([turned, turned], 1)

    def place_of(s, count=1):
        return parts.at[me, pl.ds(s, count)]

    def sem_of(s):
        return recv_sem.at[jnp.maximum(s // BATCH, s - (seqs - BATCH) + seqs // BATCH - 1)]

    def send(s):
        for d in sorted(range(1, n), key=lambda d: -min(d, n - d)):
            pltpu.make_async_remote_copy(
                src_ref=parts.at[me, s],
                dst_ref=parts.at[me, s],
                send_sem=send_sem,
                recv_sem=sem_of(s),
                device_id={"sp": lax.rem(me + d, n)},
            ).start()

    def wait_parts(s, count=1):
        place = parts.at[pl.ds(0, n - 1), pl.ds(s, count)]
        pltpu.make_async_copy(place, place, sem_of(s)).wait()

    def shares(tiles, total, high):
        highs = [jnp.broadcast_to(t[:, high : high + 1], t.shape) for t in tiles]
        top = functools.reduce(jnp.maximum, highs)
        factors = [jnp.exp(h - top) for h in highs]
        sums = [f * t for f, t in zip(factors, tiles)]
        whole = functools.reduce(jnp.add, sums)
        return factors, whole, jnp.broadcast_to(whole[:, total : total + 1], whole.shape)

    run = head // 4

    def combine(s):
        _, whole, total = shares([parts[p, s] for p in range(n)], head, head + run)
        out_ref[s] = (whole / total)[:, :head].astype(out_ref.dtype)

    def block(s, state):
        weights, total, high = state
        coming = weights_of(s + 1)
        lanes = seen_of(s, weights)
        for first, value in zip(range(head, 2 * head, run), (total, high, coming[1], coming[2])):
            lanes = jnp.where(lane < first, lanes, value)
        parts[me, s] = lanes
        return coming

    def early(s, state):
        need(s)
        state = block(s, state)
        send(s)
        return state

    def later(s, state):
        done = s - 1 - LAG

        @pl.when(lax.rem(done, BATCH) == 0)
        def _():
            wait_parts(done, BATCH)

        need(s)
        combine(done)
        state = block(s, state)
        send(s)
        return state

    fetch_q.wait()
    fetch_k(0).wait()
    state = weights_of(0)
    pl.semaphore_wait(barrier, n - 1)
    state = lax.fori_loop(0, 1 + LAG, early, state)
    state = lax.fori_loop(1 + LAG, last, later, state)

    fetch_v(last).wait()
    parts[me, last] = seen_of(last, state[0])
    send(last)
    for s in range(last - 1 - LAG, last):
        if s >= seqs - BATCH:
            wait_parts(s)
        elif s % BATCH == 0:
            wait_parts(s, BATCH)
        combine(s)
    factors, _, total = shares([parts[p, last - 1] for p in range(n)], head + 2 * run, head + 3 * run)
    factors = [f / total for f in factors]
    wait_parts(last)
    whole = functools.reduce(jnp.add, [f * parts[p, last] for p, f in enumerate(factors)])
    out_ref[last] = whole[:, :head].astype(out_ref.dtype)
    pltpu.make_async_copy(parts.at[pl.ds(0, n - 1)], parts.at[pl.ds(0, n - 1)], send_sem).wait()


def solution(mesh):
    n = mesh.shape["sp"]

    def step(q, k, v):
        seqs, tokens, heads, head = k.shape
        k = jnp.transpose(k, (0, 2, 3, 1)).reshape(seqs, heads * head, tokens)
        v = jnp.transpose(v, (0, 2, 3, 1)).reshape(seqs, heads * head, tokens)
        return pl.pallas_call(
            functools.partial(kernel, n, head**-0.5),
            out_shape=jax.ShapeDtypeStruct(q.shape, q.dtype),
            in_specs=[pl.BlockSpec(memory_space=pl.ANY)] * 3,
            out_specs=pl.BlockSpec(memory_space=pltpu.VMEM),
            scratch_shapes=[
                pltpu.VMEM(q.shape, q.dtype),
                pltpu.VMEM((SLOTS, heads * head, tokens), k.dtype),
                pltpu.VMEM((SLOTS, heads * head, tokens), v.dtype),
                pltpu.VMEM((n, seqs, heads, 128), jnp.float32),
                pltpu.SemaphoreType.DMA,
                pltpu.SemaphoreType.DMA((SLOTS,)),
                pltpu.SemaphoreType.DMA((SLOTS,)),
                pltpu.SemaphoreType.DMA,
                pltpu.SemaphoreType.DMA((seqs // BATCH - 1 + BATCH,)),
            ],
            compiler_params=pltpu.CompilerParams(
                collective_id=0, has_side_effects=True, vmem_limit_bytes=30 * 1024 * 1024
            ),
            cost_estimate=pl.CostEstimate(
                flops=4 * seqs * tokens * heads * head,
                bytes_accessed=2 * k.size * k.dtype.itemsize,
                transcendentals=seqs * heads * tokens,
            ),
        )(pltpu.with_memory_space_constraint(q, pltpu.HBM), k, v)

    return jax.shard_map(
        step,
        mesh=mesh,
        in_specs=(P("dp", None, None), P("dp", "sp", None, None), P("dp", "sp", None, None)),
        out_specs=P("dp", None, None),
        check_vma=False,
    )
```

time: 47.9 us -> 47.5 us (level)
  no operation moved by 1% of the time
where the time goes in v4:
time: 47.5 us
  Pallas kernels  46.8 us (99%)
  local copies, waits for them, and re-layouts  0.66 us (1%)
    pallas_call x1, Pallas kernels, step(): pl.pallas_call(functools.partial(kernel, n, head ** (-0.5)), out_shape=ja...  46.8 us

profile of v4, /device:TPU:113, one launch (start us, length us, event | category | flops | bytes accessed | tf_op | source)
XLA Modules:
  0.0 47.5 jit_solution(10615056747582336650)
XLA Ops:
  0.0 46.8 %shard_map.37 = bf16[32,16,64]{2,1,0:T(8,128)(2,1)S(1)} custom-call(bf16[32,16,64]{2,1,0:T(8,128)(2,1)} %q_hbm.1, bf16[32,1024,1024]{2,1,0:T(8,128)(2,1)} %bitcast.1.k_hbm, bf16[32,1024,1024]{2,1,0:T(8,128)(2,1)} %bitcast.3.v_hbm), custom_call_target="tpu_custom_call" | custom-call | flops 134217728 | bytes 134217728 | tf_op jit(solution)/shard_map/pallas_call | solution.py:180
  46.8 0.7 %copy.5 = bf16[32,16,64]{2,1,0:T(8,128)(2,1)} copy(bf16[32,16,64]{2,1,0:T(8,128)(2,1)S(1)} %shard_map.37) | data formatting | bytes 131072

commit v5 on v4

--- a/solution.py
+++ b/solution.py
@@ -9,8 +9,9 @@
 
 SLOTS = 3
 ASIDE = 8
-LAG = 7
-BATCH = 4
+LAG = 9
+BATCH = 6
+ALONE = 2
 
 
 def kernel(n, scale, q_hbm, k_hbm, v_hbm, out_ref, q_ref, k_buf, v_buf, parts, q_sem, k_sem, v_sem, send_sem, recv_sem):
@@ -18,17 +19,19 @@
     seqs, heads, head = q_ref.shape
     width = heads * head
     last = seqs - 1
-
-    def fetch_k(s):
-        slot = lax.rem(s, SLOTS)
-        return pltpu.make_async_copy(k_hbm.at[s], k_buf.at[slot], k_sem.at[slot])
-
-    def fetch_v(s):
-        slot = lax.rem(s, SLOTS)
-        return pltpu.make_async_copy(v_hbm.at[s], v_buf.at[slot], v_sem.at[slot])
-
-    for copy in fetch_k(0), fetch_k(1), fetch_v(0), fetch_k(2), fetch_v(1):
-        copy.start(priority=1)
+    cut = (heads - ASIDE) * head
+
+    def fetch(hbm, buf, sem, s, piece):
+        rows = width // sem.shape[1]
+        slot, place = lax.rem(s, SLOTS), pl.ds(piece * rows, rows)
+        return pltpu.make_async_copy(hbm.at[s, place], buf.at[slot, place], sem.at[slot, piece])
+
+    fetch_k = [functools.partial(fetch, k_hbm, k_buf, k_sem, piece=p) for p in range(k_sem.shape[1])]
+    fetch_v = [functools.partial(fetch, v_hbm, v_buf, v_sem, piece=p) for p in range(v_sem.shape[1])]
+
+    for s, copies in (0, fetch_k), (1, fetch_k), (0, fetch_v), (2, fetch_k), (1, fetch_v):
+        for copy in copies:
+            copy(s).start(priority=1)
     fetch_q = pltpu.make_async_copy(q_hbm, q_ref, q_sem)
     fetch_q.start()
 
@@ -36,25 +39,21 @@
     for d in range(1, n):
         pl.semaphore_signal(barrier, inc=1, device_id={"sp": lax.rem(me + d, n)})
 
-    def need(s):
-        fetch_k(s + 1).wait()
-
-        @pl.when(s + 3 < seqs)
+    def turn(s, fetch, ahead):
+        fetch(s).wait()
+
+        @pl.when(s + ahead < seqs)
         def _():
-            fetch_k(s + 3).start(priority=1)
-
-        fetch_v(s).wait()
-
-        @pl.when(s + 2 < seqs)
-        def _():
-            fetch_v(s + 2).start(priority=1)
-
-    def weights_of(s):
+            fetch(s + ahead).start(priority=1)
+
+    def scores_of(s):
         q = q_ref[s]
         row = lax.broadcasted_iota(jnp.int32, (heads, width), 0)
         owner = lax.broadcasted_iota(jnp.int32, (heads, width), 1) // head
         diagonal = jnp.where(owner == row, jnp.concatenate([q] * heads, axis=1), jnp.zeros((), q.dtype))
-        scores = jnp.dot(diagonal, k_buf[lax.rem(s, SLOTS)], preferred_element_type=jnp.float32) * scale
+        return jnp.dot(diagonal, k_buf[lax.rem(s, SLOTS)], preferred_element_type=jnp.float32) * scale
+
+    def weights_of(scores):
         high = jnp.max(scores, -1, keepdims=True)
         weights = jnp.exp(scores - high)
         return weights.astype(v_buf.dtype), jnp.sum(weights, -1, keepdims=True), high
@@ -63,15 +62,17 @@
     row = lax.broadcasted_iota(jnp.int32, (heads, 128), 0)
     per = 128 // head
 
-    def seen_of(s, weights):
-        slot, cut = lax.rem(s, SLOTS), (heads - ASIDE) * head
+    def low_of(s, weights):
         every = lax.dot_general(
-            weights, v_buf[slot, :cut], (((1,), (1,)), ((), ())), preferred_element_type=jnp.float32
+            weights, v_buf[lax.rem(s, SLOTS), :cut], (((1,), (1,)), ((), ())), preferred_element_type=jnp.float32
         )
         seen = jnp.zeros((heads, 128), jnp.float32)
         for j in range(cut // 128):
             seen = jnp.where(lane // head + per * j == row, every[:, 128 * j : 128 * j + 128], seen)
-        seen = seen + pltpu.roll(seen, head, 1)
+        return seen + pltpu.roll(seen, head, 1)
+
+    def high_of(s, weights):
+        slot = lax.rem(s, SLOTS)
         wide = weights.astype(jnp.float32)
         column = lax.broadcasted_iota(jnp.int32, (head, 128), 1)
         turned = jnp.zeros((head, 128), jnp.float32)
@@ -82,13 +83,10 @@
             ]
             turned = jnp.where(column == h, jnp.sum(functools.reduce(jnp.add, terms), 1, keepdims=True), turned)
         turned = turned.T[:heads]
-        return seen + jnp.concatenate([turned, turned], 1)
-
-    def place_of(s, count=1):
-        return parts.at[me, pl.ds(s, count)]
+        return jnp.concatenate([turned, turned], 1)
 
     def sem_of(s):
-        return recv_sem.at[jnp.maximum(s // BATCH, s - (seqs - BATCH) + seqs // BATCH - 1)]
+        return recv_sem.at[jnp.maximum(s // BATCH, s - (seqs - ALONE) + (seqs - ALONE) // BATCH)]
 
     def send(s):
         for d in sorted(range(1, n), key=lambda d: -min(d, n - d)):
@@ -118,20 +116,23 @@
         _, whole, total = shares([parts[p, s] for p in range(n)], head, head + run)
         out_ref[s] = (whole / total)[:, :head].astype(out_ref.dtype)
 
-    def block(s, state):
+    def block(s, state, done=None):
         weights, total, high = state
-        coming = weights_of(s + 1)
-        lanes = seen_of(s, weights)
+        for copy in fetch_k:
+            turn(s + 1, copy, 2)
+        scores = scores_of(s + 1)
+        if done is not None:
+            combine(done)
+        for copy in fetch_v:
+            turn(s, copy, 2)
+        seen = high_of(s, weights)
+        coming = weights_of(scores)
+        lanes = low_of(s, weights) + seen
         for first, value in zip(range(head, 2 * head, run), (total, high, coming[1], coming[2])):
             lanes = jnp.where(lane < first, lanes, value)
         parts[me, s] = lanes
+        send(s)
         return coming
-
-    def early(s, state):
-        need(s)
-        state = block(s, state)
-        send(s)
-        return state
 
     def later(s, state):
         done = s - 1 - LAG
@@ -140,24 +141,23 @@
         def _():
             wait_parts(done, BATCH)
 
-        need(s)
-        combine(done)
-        state = block(s, state)
-        send(s)
-        return state
+        return block(s, state, done)
 
     fetch_q.wait()
-    fetch_k(0).wait()
-    state = weights_of(0)
+    for copy in fetch_k:
+        copy(0).wait()
+    state = weights_of(scores_of(0))
     pl.semaphore_wait(barrier, n - 1)
-    state = lax.fori_loop(0, 1 + LAG, early, state)
+    state = lax.fori_loop(0, 1 + LAG, block, state)
     state = lax.fori_loop(1 + LAG, last, later, state)
 
-    fetch_v(last).wait()
-    parts[me, last] = seen_of(last, state[0])
+    for copy in fetch_v:
+        copy(last).wait()
+    seen = high_of(last, state[0])
+    parts[me, last] = seen + low_of(last, state[0])
     send(last)
     for s in range(last - 1 - LAG, last):
-        if s >= seqs - BATCH:
+        if s >= seqs - ALONE:
             wait_parts(s)
         elif s % BATCH == 0:
             wait_parts(s, BATCH)
@@ -188,10 +188,10 @@
                 pltpu.VMEM((SLOTS, heads * head, tokens), v.dtype),
                 pltpu.VMEM((n, seqs, heads, 128), jnp.float32),
                 pltpu.SemaphoreType.DMA,
-                pltpu.SemaphoreType.DMA((SLOTS,)),
-                pltpu.SemaphoreType.DMA((SLOTS,)),
+                pltpu.SemaphoreType.DMA((SLOTS, 1)),
+                pltpu.SemaphoreType.DMA((SLOTS, 2)),
                 pltpu.SemaphoreType.DMA,
-                pltpu.SemaphoreType.DMA((seqs // BATCH - 1 + BATCH,)),
+                pltpu.SemaphoreType.DMA(((seqs - ALONE) // BATCH + ALONE,)),
             ],
             compiler_params=pltpu.CompilerParams(
                 collective_id=0, has_side_effects=True, vmem_limit_bytes=30 * 1024 * 1024

time: 47.5 us -> 47.1 us (level)
  no operation moved by 1% of the time
where the time goes in v5:
time: 47.1 us; the launch traced here: 47 us
  Pallas kernels  46.4 us (99%)
  local copies, waits for them, and re-layouts  0.66 us (1%)
    pallas_call x1, Pallas kernels, step(): pl.pallas_call(functools.partial(kernel, n, head ** (-0.5)), out_shape=ja...  46.4 us

profile of v5, /device:TPU:113, one launch (start us, length us, event | category | flops | bytes accessed | tf_op | source)
XLA Modules:
  0.0 47.0 jit_solution(11173272664727626620)
XLA Ops:
  0.0 46.4 %shard_map.37 = bf16[32,16,64]{2,1,0:T(8,128)(2,1)S(1)} custom-call(bf16[32,16,64]{2,1,0:T(8,128)(2,1)} %q_hbm.1, bf16[32,1024,1024]{2,1,0:T(8,128)(2,1)} %bitcast.1.k_hbm, bf16[32,1024,1024]{2,1,0:T(8,128)(2,1)} %bitcast.3.v_hbm), custom_call_target="tpu_custom_call" | custom-call | flops 134217728 | bytes 134217728 | tf_op jit(solution)/shard_map/pallas_call | solution.py:180
  46.4 0.7 %copy.5 = bf16[32,16,64]{2,1,0:T(8,128)(2,1)} copy(bf16[32,16,64]{2,1,0:T(8,128)(2,1)S(1)} %shard_map.37) | data formatting | bytes 131072

commit v6 on v5

--- a/solution.py
+++ b/solution.py
@@ -14,7 +14,7 @@
 ALONE = 2
 
 
-def kernel(n, scale, q_hbm, k_hbm, v_hbm, out_ref, q_ref, k_buf, v_buf, parts, q_sem, k_sem, v_sem, send_sem, recv_sem):
+def kernel(n, scale, q_hbm, k_hbm, v_hbm, out_ref, q_ref, k_buf, v_buf, parts, ends, q_sem, k_sem, v_sem, send_sem, recv_sem):
     me = lax.axis_index("sp")
     seqs, heads, head = q_ref.shape
     width = heads * head
@@ -88,13 +88,13 @@
     def sem_of(s):
         return recv_sem.at[jnp.maximum(s // BATCH, s - (seqs - ALONE) + (seqs - ALONE) // BATCH)]
 
-    def send(s):
+    def send(place, send_sem, recv_sem):
         for d in sorted(range(1, n), key=lambda d: -min(d, n - d)):
             pltpu.make_async_remote_copy(
-                src_ref=parts.at[me, s],
-                dst_ref=parts.at[me, s],
+                src_ref=place,
+                dst_ref=place,
                 send_sem=send_sem,
-                recv_sem=sem_of(s),
+                recv_sem=recv_sem,
                 device_id={"sp": lax.rem(me + d, n)},
             ).start()
 
@@ -131,7 +131,7 @@
         for first, value in zip(range(head, 2 * head, run), (total, high, coming[1], coming[2])):
             lanes = jnp.where(lane < first, lanes, value)
         parts[me, s] = lanes
-        send(s)
+        send(parts.at[me, s], send_sem.at[0], sem_of(s))
         return coming
 
     def later(s, state):
@@ -154,8 +154,8 @@
     for copy in fetch_v:
         copy(last).wait()
     seen = high_of(last, state[0])
-    parts[me, last] = seen + low_of(last, state[0])
-    send(last)
+    ends[me] = (seen + low_of(last, state[0])).astype(ends.dtype)
+    send(ends.at[me], send_sem.at[1], sem_of(last))
     for s in range(last - 1 - LAG, last):
         if s >= seqs - ALONE:
             wait_parts(s)
@@ -164,10 +164,13 @@
         combine(s)
     factors, _, total = shares([parts[p, last - 1] for p in range(n)], head + 2 * run, head + 3 * run)
     factors = [f / total for f in factors]
-    wait_parts(last)
-    whole = functools.reduce(jnp.add, [f * parts[p, last] for p, f in enumerate(factors)])
+    all_ends = ends.at[pl.ds(0, n - 1)]
+    pltpu.make_async_copy(all_ends, all_ends, sem_of(last)).wait()
+    whole = functools.reduce(jnp.add, [f * ends[p].astype(jnp.float32) for p, f in enumerate(factors)])
     out_ref[last] = whole[:, :head].astype(out_ref.dtype)
-    pltpu.make_async_copy(parts.at[pl.ds(0, n - 1)], parts.at[pl.ds(0, n - 1)], send_sem).wait()
+    all_parts = parts.at[pl.ds(0, n - 1)]
+    pltpu.make_async_copy(all_parts, all_parts, send_sem.at[0]).wait()
+    pltpu.make_async_copy(all_ends, all_ends, send_sem.at[1]).wait()
 
 
 def solution(mesh):
@@ -186,11 +189,12 @@
                 pltpu.VMEM(q.shape, q.dtype),
                 pltpu.VMEM((SLOTS, heads * head, tokens), k.dtype),
                 pltpu.VMEM((SLOTS, heads * head, tokens), v.dtype),
-                pltpu.VMEM((n, seqs, heads, 128), jnp.float32),
+                pltpu.VMEM((n, seqs - 1, heads, 128), jnp.float32),
+                pltpu.VMEM((n, heads, 128), q.dtype),
                 pltpu.SemaphoreType.DMA,
                 pltpu.SemaphoreType.DMA((SLOTS, 1)),
                 pltpu.SemaphoreType.DMA((SLOTS, 2)),
-                pltpu.SemaphoreType.DMA,
+                pltpu.SemaphoreType.DMA((2,)),
                 pltpu.SemaphoreType.DMA(((seqs - ALONE) // BATCH + ALONE,)),
             ],
             compiler_params=pltpu.CompilerParams(

time: 47.1 us -> 47.1 us (level)
  no operation moved by 1% of the time
where the time goes in v6:
time: 47.1 us; the launch traced here: 47 us
  Pallas kernels  46.3 us (98%)
  local copies, waits for them, and re-layouts  0.66 us (1%)
    pallas_call x1, Pallas kernels, step(): pl.pallas_call(functools.partial(kernel, n, head ** (-0.5)), out_shape=ja...  46.3 us

profile of v6, /device:TPU:113, one launch (start us, length us, event | category | flops | bytes accessed | tf_op | source)
XLA Modules:
  0.0 47.0 jit_solution(10307556066232876605)
XLA Ops:
  0.0 46.3 %shard_map.37 = bf16[32,16,64]{2,1,0:T(8,128)(2,1)S(1)} custom-call(bf16[32,16,64]{2,1,0:T(8,128)(2,1)} %q_hbm.1, bf16[32,1024,1024]{2,1,0:T(8,128)(2,1)} %bitcast.1.k_hbm, bf16[32,1024,1024]{2,1,0:T(8,128)(2,1)} %bitcast.3.v_hbm), custom_call_target="tpu_custom_call" | custom-call | flops 134217728 | bytes 134217728 | tf_op jit(solution)/shard_map/pallas_call | solution.py:183
  46.4 0.7 %copy.5 = bf16[32,16,64]{2,1,0:T(8,128)(2,1)} copy(bf16[32,16,64]{2,1,0:T(8,128)(2,1)S(1)} %shard_map.37) | data formatting | bytes 131072
